TPU v7x, 256 devices: a whole 4x4x8 slice. The times are simulated.
256 devices in a mesh: ch: 128 (over x, y_lo, z, core), rep: 2 (over y_hi).
Axes of the slice: x: 4, y: 4 (y_hi: 2, y_lo: 2; y = y_hi * 2 + y_lo), z: 8, core: 2. Of those that a mesh axis runs over, the one named last changes fastest.
Arguments:
- fields_a: bfloat16 [32, 128, 32768], P('rep', 'ch'), parts along dimension 0, may hold values from -6 to 6
- latent_b: bfloat16 [32, 16384, 512], P('rep', 'ch'), parts along dimension 0, may hold values from -6 to 6
- regrid_w: bfloat16 [256, 1, 128, 64], replicated, may hold values from -0.5 to 0.5
- cell_tiles: int32 [256, 1], replicated, may hold values from 0 to 255, as said below
- norm_a: float32 [128], replicated, may hold values from 0.5 to 1.5
- enc_in: bfloat16 [128, 512], replicated, may hold values from -0.5 to 0.5
- enc_mid: bfloat16 [512, 512], replicated, may hold values from -0.25 to 0.25
- enc_out: bfloat16 [512, 512], replicated, may hold values from -0.25 to 0.25
- norm_b: float32 [512], replicated, may hold values from 0.5 to 1.5
- dec_mid: bfloat16 [512, 512], replicated, may hold values from -0.25 to 0.25
- dec_out: bfloat16 [512, 128], replicated, may hold values from -0.25 to 0.25
Outputs:
- latent_a: bfloat16 [32, 16384, 512], P('rep', 'ch'), parts along dimension 0
- cells_b: bfloat16 [32, 128, 32768], P('rep', 'ch'), parts along dimension 0
There are 2 independent parts, one for each index of `rep`. A program takes and returns all parts, laid end to end along the dimension named above; an argument that names none is the same for every part. Nothing has to cross between parts.
Inputs may be any that keep to these rules, and one draw needn't show every extreme that they name: The one column of cell_tiles names every one of the 256 cell blocks exactly once.
All inputs are finite; a program needn't handle non-finite values.
Results may differ from a plain program's by a relative error of at most 0.0066.
Values may be sent and summed in bfloat16 or wider, within the bound.
No kernel may reach another device: no remote copies, remote signals or barrier semaphores. Data moves between devices by JAX's collectives and lax.ppermute only.
A program may use at most 64 MiB of HBM per device.

v0:
```python
import jax
import jax.numpy as jnp
from jax import lax
from jax.sharding import PartitionSpec as P

BN = 64
BC = 128
K = 1


EPSILON = 1e-05


def normalize(values, gain_vec, along):
    average = jnp.mean(values, axis=along, keepdims=True)
    centred = values - average
    spread = jnp.mean(centred * centred, axis=along, keepdims=True)
    return centred * lax.rsqrt(spread + EPSILON) * gain_vec


def shards(
    fields_a,
    latent_b,
    regrid_w,
    cell_tiles,
    norm_a,
    enc_in,
    enc_mid,
    enc_out,
    norm_b,
    dec_mid,
    dec_out,
):
    groups = lax.axis_size("ch")
    samples = fields_a.shape[0]
    own_channels = fields_a.shape[1]
    blocks_all = cell_tiles.shape[0]
    node_rows = latent_b.shape[1]
    hidden = latent_b.shape[2]
    channels = own_channels * groups
    blocks = fields_a.reshape(samples, own_channels, blocks_all, BC)
    chosen = jnp.take(blocks, cell_tiles, axis=2).reshape(samples, own_channels, blocks_all, K * BC)
    weights = regrid_w.reshape(blocks_all, K * BC, BN)
    grid_vals = jnp.einsum("ecnj,njm->ecnm", chosen, weights, preferred_element_type=jnp.float32)
    grid_sent = grid_vals.astype(jnp.bfloat16).reshape(samples, own_channels, groups, node_rows)
    received_a = lax.all_to_all(grid_sent, "ch", split_axis=2, concat_axis=1, tiled=True)
    normed = normalize(latent_b.astype(jnp.float32), norm_b, 2).astype(jnp.bfloat16)
    middle = jax.nn.silu(
        jnp.einsum("enh,hg->eng", normed, dec_mid, preferred_element_type=jnp.float32)
    ).astype(jnp.bfloat16)
    out_split = dec_out.reshape(hidden, groups, own_channels)
    decoded_sent = jnp.einsum(
        "enh,hjc->ecjn", middle, out_split, preferred_element_type=jnp.float32
    ).astype(jnp.bfloat16)
    values = received_a.reshape(samples, channels, node_rows).astype(jnp.float32)
    normed = normalize(values, norm_a[:, None], 1).astype(jnp.bfloat16)
    base = jnp.einsum("ecn,ch->enh", normed, enc_in, preferred_element_type=jnp.float32).astype(
        jnp.bfloat16
    )
    middle = jax.nn.silu(
        jnp.einsum("enh,hg->eng", base, enc_mid, preferred_element_type=jnp.float32)
    ).astype(jnp.bfloat16)
    result = base.astype(jnp.float32) + jnp.einsum(
        "enh,hg->eng", middle, enc_out, preferred_element_type=jnp.float32
    )
    latent_a = result.astype(jnp.bfloat16)
    received_b = lax.all_to_all(decoded_sent, "ch", split_axis=2, concat_axis=1, tiled=True)
    node_blocks = jnp.moveaxis(received_b, 1, 2).reshape(samples, own_channels, blocks_all, BN)
    inverse = jnp.argsort(cell_tiles, axis=0).T
    picked = jnp.take(node_blocks, inverse, axis=2)
    weight_sel = regrid_w[inverse, jnp.arange(K)[:, None]]
    total = jnp.einsum("ecknm,knbm->ecnb", picked, weight_sel, preferred_element_type=jnp.float32)
    cells_b = total.astype(jnp.bfloat16).reshape(samples, own_channels, blocks_all * BC)
    return (latent_a, cells_b)


def solution(mesh):
    placed = (
        P("rep", "ch", None),
        P("rep", "ch", None),
        P(),
        P(),
        P(),
        P(),
        P(),
        P(),
        P(),
        P(),
        P(),
    )
    return jax.shard_map(
        shards,
        mesh=mesh,
        in_specs=placed,
        out_specs=(P("rep", "ch", None), P("rep", "ch", None)),
        check_vma=False,
    )
```

profile of v0, /device:TPU:1, one launch (start us, length us, event | category | flops | bytes accessed | tf_op | source)
XLA Modules:
  0.0 80.6 jit_solution(7968910179275049129)
XLA Ops:
  0.6 0.0 copy-start
  0.6 0.0 copy-start.1
  0.7 0.0 copy-start.6
  0.7 0.0 copy-start.7
  0.7 2.1 %convert_reduce_fusion = f32[16,128]{1,0:T(8,128)S(1)} fusion(bf16[16,128,512]{2,1,0:T(8,128)(2,1)} %param.12), kind=kLoop, calls=%fused_computation.4 | loop fusion | flops 2095104 | bytes 2105344 | tf_op jit(solution)/shard_map/reduce_sum | solution.py:15
  2.8 2.5 %fusion.2 = f32[16,128]{1,0:T(8,128)S(1)} fusion(bf16[16,128,512]{2,1,0:T(8,128)(2,1)} %param.12, f32[16,128]{1,0:T(8,128)S(1)} %broadcast_multiply_fusion), kind=kLoop, calls=%fused_computation.7 | loop fusion | flops 4192256 | bytes 2113536 | tf_op jit(solution)/shard_map/reduce_sum | solution.py:17
  5.3 0.0 copy-done.1
  5.3 0.0 copy-done.6
  5.3 0.0 copy-done.7
  5.3 3.4 %fusion.27 = bf16[16,1,128,128]{2,3,0,1:T(8,128)(2,1)S(1)} fusion(bf16[16,128,512]{2,1,0:T(8,128)(2,1)S(1)} %copy-done.1, f32[512]{0:T(512)S(1)} %copy-done.7, f32[16,128]{1,0:T(8,128)S(1)} %add_rsqrt_fusion, f32[16,128]{1,0:T(8,128)S(1)} %broadcast_multiply_fusion, bf16[512,512]{1,0:T(8,128)(2,1)} %param.20, bf16[512,128]{1,0:T(8,128)(2,1)S(1)} %copy-done.6), kind=kOutput, calls=%fused_computation.29 | convolution fusion | flops 1352925184 | bytes 3295232 | tf_op jit(solution)/shard_map/enh,hjc->ecjn/dot_general | solution.py:52
  8.7 0.0 copy-start.3
  8.7 1.2 %copy.28 = bf16[16,1,128,128]{3,0,1,2:T(8,128)(2,1)} copy(bf16[16,1,128,128]{2,3,0,1:T(8,128)(2,1)S(1)} %fusion.27) | data formatting | bytes 1048576 | tf_op jit(solution)/shard_map/convert_element_type | solution.py:54
  9.9 14.8 %all-to-all-start.1 = ((bf16[16,1,128,128]{3,0,1,2:T(8,128)(2,1)}), bf16[16,1,128,128]{3,0,1,2:T(8,128)(2,1)S(1)}, u32[]{:S(2)}, u32[]{:S(2)}) async-start(bf16[16,1,128,128]{3,0,1,2:T(8,128)(2,1)} %copy.28), calls=%async_computation.1 | async-start | bytes 1048576 | tf_op jit(solution)/shard_map/all_to_all | solution.py:67
  24.7 1.4 %copy.33 = bf16[2,8,256,128]{3,2,1,0:T(8,128)(2,1)S(1)} copy(bf16[2,8,256,128]{3,1,2,0:T(8,128)(2,1)} %bitcast.88) | data formatting | bytes 2097152
  26.1 0.7 copy.24
  26.8 0.0 copy-done.3
  26.8 0.8 %gather_fusion = bf16[256,16,128]{2,1,0:T(8,128)(2,1)S(1)} fusion(bf16[16,256,128]{2,0,1:T(8,128)(2,1)S(1)} %copy.24, s32[1024]{0:T(1024)S(1)} %pad_clamp_fusion.1), kind=kCustom, calls=%fused_computation | custom fusion | bytes 2098176 | tf_op jit(solution)/shard_map/jit(_take)/gather | solution.py:42
  27.7 4.5 %fusion.19 = bf16[16,1,256,64]{3,0,2,1:T(8,128)(2,1)S(1)} fusion(bf16[256,1,128,64]{2,3,1,0:T(8,128)(2,1)} %param.13, bf16[256,16,128]{2,1,0:T(8,128)(2,1)S(1)} %gather_fusion, pred[256]{0:T(512)(128)(4,1)S(1)} %get-tuple-element.4), kind=kOutput, calls=%fused_computation.25 | convolution fusion | flops 67895296 | bytes 5767424 | tf_op jit(solution)/shard_map/ecnj,njm->ecnm/dot_general | solution.py:44
  32.2 0.3 copy.25
  32.5 0.5 reshape.155
  33.0 1.1 %copy.26 = bf16[16,1,128,128]{3,0,1,2:T(8,128)(2,1)} copy(bf16[16,1,128,128]{3,2,0,1:T(8,128)(2,1)S(1)} %reshape.155) | data formatting | bytes 1048576 | tf_op jit(solution)/shard_map/reshape | solution.py:45
  34.1 10.5 %all-to-all-done.1 = bf16[16,1,128,128]{3,0,1,2:T(8,128)(2,1)S(1)} async-done(((bf16[16,1,128,128]{3,0,1,2:T(8,128)(2,1)}), bf16[16,1,128,128]{3,0,1,2:T(8,128)(2,1)S(1)}, u32[]{:S(2)}, u32[]{:S(2)}) %all-to-all-start.1) | async-done | bytes 524320 | tf_op jit(solution)/shard_map/all_to_all | solution.py:67
  44.6 5.5 %all-to-all-start = ((bf16[16,1,128,128]{3,0,1,2:T(8,128)(2,1)}), bf16[16,1,128,128]{3,0,1,2:T(8,128)(2,1)S(1)}, u32[]{:S(2)}, u32[]{:S(2)}) async-start(bf16[16,1,128,128]{3,0,1,2:T(8,128)(2,1)} %copy.26), calls=%async_computation | async-start | bytes 1048576 | tf_op jit(solution)/shard_map/all_to_all | solution.py:46
  50.1 3.2 %sort.17 = (s32[256,1]{0,1:T(1,128)}, s32[256,1]{0,1:T(1,128)S(1)}) sort(s32[256,1]{0,1:T(1,128)S(1)} %copy-done.3, s32[256,1]{0,1:T(1,128)S(1)} %iota.7), dimensions={0}, to_apply=%region_2.3 | sort | flops 2048 | bytes 4096 | tf_op jit(solution)/shard_map/jit(argsort)/sort | solution.py:69
  53.4 5.2 %gather_fusion.1 = bf16[256,128,64]{1,2,0:T(8,128)(2,1)} fusion(bf16[256,1,128,64]{2,3,1,0:T(8,128)(2,1)} %param.13, s32[256]{0:T(256)S(1)} %bitcast.86), kind=kCustom, calls=%fused_computation.1 | custom fusion | bytes 8390656 | tf_op jit(solution)/shard_map/gather | solution.py:71
  58.6 0.1 copy.29
  58.7 0.4 reshape.176
  59.1 0.7 copy.30
  59.8 9.9 %all-to-all-done = bf16[16,1,128,128]{3,0,1,2:T(8,128)(2,1)S(1)} async-done(((bf16[16,1,128,128]{3,0,1,2:T(8,128)(2,1)}), bf16[16,1,128,128]{3,0,1,2:T(8,128)(2,1)S(1)}, u32[]{:S(2)}, u32[]{:S(2)}) %all-to-all-start) | async-done | bytes 524320 | tf_op jit(solution)/shard_map/all_to_all | solution.py:46
  69.8 0.1 convert_reduce_fusion.1
  69.9 0.2 fusion.33
  70.1 0.9 %gather_fusion.2 = bf16[256,16,64]{2,1,0:T(8,128)(2,1)S(1)} fusion(bf16[16,256,64]{2,0,1:T(8,128)(2,1)S(1)} %copy.30, s32[1024]{0:T(1024)S(1)} %pad_clamp_fusion), kind=kCustom, calls=%fused_computation.2 | custom fusion | bytes 1049600 | tf_op jit(solution)/shard_map/jit(_take)/gather | solution.py:70
  71.0 0.0 copy-start.4
  71.0 0.0 copy-start.2
  71.0 3.5 %fusion.18 = bf16[1,256,2,8,128]{4,3,2,1,0:T(8,128)(2,1)S(1)} fusion(bf16[256,128,64]{1,2,0:T(8,128)(2,1)} %gather_fusion.1, bf16[256,16,64]{2,1,0:T(8,128)(2,1)S(1)} %gather_fusion.2, pred[256]{0:T(512)(128)(4,1)S(1)} %compare_and_fusion), kind=kOutput, calls=%fused_computation.24 | convolution fusion | flops 67895296 | bytes 5767424 | tf_op jit(solution)/shard_map/ecknm,knbm->ecnb/dot_general | solution.py:72
  74.5 0.0 copy-start.5
  74.5 1.0 %copy.37 = bf16[1,256,2,8,128]{4,3,1,2,0:T(8,128)(2,1)} copy(bf16[1,256,2,8,128]{4,3,2,1,0:T(8,128)(2,1)S(1)} %fusion.18) | data formatting | bytes 2097152 | tf_op jit(solution)/shard_map/reshape | solution.py:73
  75.5 0.0 copy-done.4
  75.5 0.2 fusion.35
  75.8 0.0 copy-done.2
  75.8 0.7 convolution_convert_fusion
  76.5 0.0 copy-done
  76.5 0.0 copy-done.5
  76.5 4.0 %add_convert_fusion = bf16[16,128,512]{2,1,0:T(8,128)(2,1)} fusion(bf16[16,128,512]{2,1,0:T(8,128)(2,1)S(1)} %convolution_convert_fusion, bf16[512,512]{1,0:T(8,128)(2,1)S(1)} %copy-done, bf16[512,512]{1,0:T(8,128)(2,1)S(1)} %copy-done.5), kind=kOutput, calls=%fused_computation.13 | convolution fusion | flops 2155872256 | bytes 5242880 | tf_op jit(solution)/shard_map/enh,hg->eng/dot_general | solution.py:63
  (12 shorter events, 0.1 us)
Async XLA Ops:
  0.6 75.9 %copy-start = (bf16[512,512]{1,0:T(8,128)(2,1)S(1)}, bf16[512,512]{1,0:T(8,128)(2,1)}, u32[]{:S(2)}) copy-start(bf16[512,512]{1,0:T(8,128)(2,1)} %param.18) | copy-start | bytes 1572868
  0.6 4.6 %copy-start.1 = (bf16[16,128,512]{2,1,0:T(8,128)(2,1)S(1)}, bf16[16,128,512]{2,1,0:T(8,128)(2,1)}, u32[]{:S(2)}) copy-start(bf16[16,128,512]{2,1,0:T(8,128)(2,1)} %param.12) | copy-start | bytes 6291460
  0.7 4.6 %copy-start.6 = (bf16[512,128]{1,0:T(8,128)(2,1)S(1)}, bf16[512,128]{1,0:T(8,128)(2,1)}, u32[]{:S(2)}) copy-start(bf16[512,128]{1,0:T(8,128)(2,1)} %param.21) | copy-start | bytes 393220
  0.7 4.6 %copy-start.7 = (f32[512]{0:T(512)S(1)}, f32[512]{0:T(512)}, u32[]{:S(2)}) copy-start(f32[512]{0:T(512)} %param.19) | copy-start | bytes 6148
  8.7 18.1 %copy-start.3 = (s32[256,1]{0,1:T(1,128)S(1)}, s32[256,1]{0,1:T(1,128)}, u32[]{:S(2)}) copy-start(s32[256,1]{0,1:T(1,128)} %param.14) | copy-start | bytes 3076
  9.9 34.7 %all-to-all-start.1 = ((bf16[16,1,128,128]{3,0,1,2:T(8,128)(2,1)}), bf16[16,1,128,128]{3,0,1,2:T(8,128)(2,1)S(1)}, u32[]{:S(2)}, u32[]{:S(2)}) async-start(bf16[16,1,128,128]{3,0,1,2:T(8,128)(2,1)} %copy.28), calls=%async_computation.1 | async-start | bytes 1048576 | tf_op jit(solution)/shard_map/all_to_all | solution.py:67
  44.6 25.2 %all-to-all-start = ((bf16[16,1,128,128]{3,0,1,2:T(8,128)(2,1)}), bf16[16,1,128,128]{3,0,1,2:T(8,128)(2,1)S(1)}, u32[]{:S(2)}, u32[]{:S(2)}) async-start(bf16[16,1,128,128]{3,0,1,2:T(8,128)(2,1)} %copy.26), calls=%async_computation | async-start | bytes 1048576 | tf_op jit(solution)/shard_map/all_to_all | solution.py:46
  71.0 4.6 %copy-start.4 = (f32[128]{0:T(128)S(1)}, f32[128]{0:T(128)}, u32[]{:S(2)}) copy-start(f32[128]{0:T(128)} %param.15) | copy-start | bytes 1540
  71.0 4.8 %copy-start.2 = (bf16[128,512]{1,0:T(8,128)(2,1)S(1)}, bf16[128,512]{1,0:T(8,128)(2,1)}, u32[]{:S(2)}) copy-start(bf16[128,512]{1,0:T(8,128)(2,1)} %param.16) | copy-start | bytes 393220
  74.5 2.0 %copy-start.5 = (bf16[512,512]{1,0:T(8,128)(2,1)S(1)}, bf16[512,512]{1,0:T(8,128)(2,1)}, u32[]{:S(2)}) copy-start(bf16[512,512]{1,0:T(8,128)(2,1)} %param.17) | copy-start | bytes 1572868
where the time goes:
time: 81 us; the launch traced here: 80.6 us
  waiting for transfers between devices  20.4 us (25%)
  starting transfers between devices  20.3 us (25%)
  matrix products  16.2 us (20%)
  local copies, waits for them, and re-layouts  14.4 us (18%)
  other arithmetic  8.38 us (10%)
  between operations  0.92 us (1%)
    all_to_all x1, starting transfers between devices, shards(): lax.all_to_all(decoded_sent, 'ch', split_axis=2, concat_axis=1, tiled=True)  14.8 us
    all_to_all x1, waiting for transfers between devices, shards(): lax.all_to_all(decoded_sent, 'ch', split_axis=2, concat_axis=1, tiled=True)  10.5 us
    all_to_all x1, waiting for transfers between devices, shards(): lax.all_to_all(grid_sent, 'ch', split_axis=2, concat_axis=1, tiled=True)  9.93 us
    all_to_all x1, starting transfers between devices, shards(): lax.all_to_all(grid_sent, 'ch', split_axis=2, concat_axis=1, tiled=True)  5.49 us
    gather x1, local copies, waits for them, and re-layouts, shards(): weight_sel = regrid_w[inverse, jnp.arange(K)[:, None]]  5.21 us
    dot_general x1, matrix products, shards(): jnp.einsum('ecnj,njm->ecnm', chosen, weights, preferred_element_type=jnp....  4.53 us
    dot_general x1, matrix products, shards(): jnp.einsum('enh,hg->eng', middle, enc_out, preferred_element_type=jnp.flo...  4.04 us
    dot_general x1, matrix products, shards(): jnp.einsum('ecknm,knbm->ecnb', picked, weight_sel, preferred_element_type...  3.5 us
  transfers between devices with their start and end apart: 2, of which 2 were waited for; matrix products, arithmetic and copies ran while one was open for 24% of the time, Pallas kernels for 0%

commit v1 on v0

v1 whole, which is shorter than its diff:
```python
import functools

import jax
import jax.numpy as jnp
from jax import lax
from jax.experimental import pallas as pl
from jax.experimental.pallas import tpu as pltpu
from jax.sharding import PartitionSpec as P

BN = 64
BC = 128
EPSILON = 1e-05
STEP = 8
DEC = 1
ENC = 1


def half_silu(values):
    half = values * 0.5
    return half + half * jnp.tanh(half)


def nt_dot(left, right):
    return lax.dot_general(left, right, (((1,), (1,)), ((), ())), preferred_element_type=jnp.float32)


def tn_dot(left, right):
    return lax.dot_general(left, right, (((0,), (0,)), ((), ())), preferred_element_type=jnp.float32)


def head_kernel(
    tiles, fields, latent, weights, gain, mid_w, out_w, sent,
    fields_v, latent_v, weights_v, mid_v, out_v, out_t, turned, sent_v, sems,
):
    samples, nodes, hidden = latent.shape
    pairs = weights.shape[0]
    steps = samples // STEP
    parts = 2
    share = pairs // parts

    def latent_copy(i):
        rows = pl.ds(i * STEP, STEP)
        return pltpu.make_async_copy(latent.at[rows], latent_v.at[rows], sems.at[i])

    def weight_copy(i):
        rows = pl.ds(i * share, share)
        return pltpu.make_async_copy(weights.at[rows], weights_v.at[rows], sems.at[steps + i])

    mid_copy = pltpu.make_async_copy(mid_w, mid_v, sems.at[steps + parts])
    out_copy = pltpu.make_async_copy(out_w, out_v, sems.at[steps + parts + 1])
    fields_copy = pltpu.make_async_copy(fields, fields_v, sems.at[steps + parts + 2])
    decoded_copy = pltpu.make_async_copy(
        sent_v.at[:, samples:, :], sent.at[:, samples:, :], sems.at[steps + parts + 3]
    )

    def sent_copy(i):
        rows = pl.ds(i * share, share)
        return pltpu.make_async_copy(
            sent_v.at[rows, :samples, :], sent.at[rows, :samples, :], sems.at[steps + parts + 4 + i]
        )

    latent_copy(0).start()
    mid_copy.start()
    out_copy.start()
    for i in range(1, steps):
        latent_copy(i).start()
    fields_copy.start()
    for i in range(parts):
        weight_copy(i).start()

    out_copy.wait()
    out_t[...] = out_v[...].T
    scale = gain[...]

    def decode(i, carry):
        latent_copy(i).wait()
        values = latent_v[pl.ds(i * STEP, STEP)].reshape(STEP * nodes, hidden).astype(jnp.float32)
        centred = values - jnp.mean(values, axis=1, keepdims=True)
        spread = jnp.mean(centred * centred, axis=1, keepdims=True)
        normed = (centred * lax.rsqrt(spread + EPSILON) * scale).astype(jnp.bfloat16)
        middle = half_silu(
            jnp.dot(normed, mid_v[...], preferred_element_type=jnp.float32)
        ).astype(jnp.bfloat16)
        result = nt_dot(out_t[...], middle)
        for s in range(STEP):
            turned[:, i * STEP + s, :] = result[:, s * nodes:(s + 1) * nodes]
        return carry

    mid_copy.wait()
    lax.fori_loop(0, steps, decode, 0, unroll=DEC)
    sent_v[:, samples:, :] = turned[...].astype(jnp.bfloat16)
    decoded_copy.start()

    fields_copy.wait()
    low = lax.broadcasted_iota(jnp.int32, (samples, BC), 1) < BN

    for part in range(parts):
        weight_copy(part).wait()

        def regrid(d, carry):
            first = pl.multiple_of(tiles[2 * d] * BC, BC)
            second = pl.multiple_of(tiles[2 * d + 1] * BC, BC)
            chosen = jnp.concatenate(
                [fields_v[:, pl.ds(first, BC)], fields_v[:, pl.ds(second, BC)]], axis=0
            )
            both = nt_dot(chosen, weights_v[d])
            sent_v[d, :samples, :] = jnp.where(low, both[:samples], both[samples:]).astype(jnp.bfloat16)
            return carry

        lax.fori_loop(part * share, (part + 1) * share, regrid, 0, unroll=64)
        sent_copy(part).start()

    decoded_copy.wait()
    for part in range(parts):
        sent_copy(part).wait()


def tail_kernel(
    tiles, got, weights, gain, in_w, mid_w, out_w, latent, cells,
    weights_v, turned, latent_v, cells_v, sems,
):
    samples, nodes, hidden = latent.shape
    pairs = weights.shape[0]
    steps = samples // STEP
    parts = 2
    share = pairs // parts

    def latent_copy(i):
        rows = pl.ds(i * STEP, STEP)
        return pltpu.make_async_copy(latent_v.at[rows], latent.at[rows], sems.at[i])

    def weight_copy(i):
        rows = pl.ds(i * share, share)
        return pltpu.make_async_copy(weights.at[rows], weights_v.at[rows], sems.at[steps + i])

    cells_copy = pltpu.make_async_copy(cells_v, cells, sems.at[steps + parts])
    for i in range(parts):
        weight_copy(i).start()

    values = got[:, :samples, :].astype(jnp.float32)
    average = jnp.mean(values, axis=0, keepdims=True)
    centred = values - average
    spread = jnp.mean(centred * centred, axis=0, keepdims=True)
    turned[...] = centred * lax.rsqrt(spread + EPSILON)

    scale = jnp.broadcast_to(gain[...], (pairs, nodes))

    def encode(i, carry):
        bases = []
        for s in range(STEP):
            normed = (turned[:, i * STEP + s, :] * scale).astype(jnp.bfloat16)
            bases.append(tn_dot(normed, in_w[...]))
        base = jnp.concatenate(bases, axis=0).astype(jnp.bfloat16)
        middle = half_silu(
            jnp.dot(base, mid_w[...], preferred_element_type=jnp.float32)
        ).astype(jnp.bfloat16)
        result = base.astype(jnp.float32) + jnp.dot(
            middle, out_w[...], preferred_element_type=jnp.float32
        )
        latent_v[pl.ds(i * STEP, STEP)] = result.astype(jnp.bfloat16).reshape(STEP, nodes, hidden)
        latent_copy(i).start()
        return carry

    lax.fori_loop(0, steps // 2, encode, 0, unroll=ENC)
    low = lax.broadcasted_iota(jnp.int32, (samples, BC), 1) < BN
    for part in range(parts):
        weight_copy(part).wait()

        def spread_out(d, carry):
            first = pl.multiple_of(tiles[2 * d] * BC, BC)
            second = pl.multiple_of(tiles[2 * d + 1] * BC, BC)
            node = got[d, samples:, :].astype(jnp.float32)
            stacked = jnp.concatenate(
                [jnp.where(low, node, 0.0), jnp.where(low, 0.0, node)], axis=0
            ).astype(jnp.bfloat16)
            both = jnp.dot(stacked, weights_v[d], preferred_element_type=jnp.float32).astype(jnp.bfloat16)
            cells_v[:, pl.ds(first, BC)] = both[:samples]
            cells_v[:, pl.ds(second, BC)] = both[samples:]
            return carry

        lax.fori_loop(part * share, (part + 1) * share, spread_out, 0, unroll=64)
    cells_copy.start()

    lax.fori_loop(steps // 2, steps, encode, 0, unroll=ENC)
    cells_copy.wait()
    for i in range(steps):
        latent_copy(i).wait()


def shards(
    fields_a, latent_b, regrid_w, cell_tiles, norm_a,
    enc_in, enc_mid, enc_out, norm_b, dec_mid, dec_out,
):
    samples, _, cell_count = fields_a.shape
    nodes, hidden = latent_b.shape[1:]
    blocks = cell_tiles.shape[0]
    pairs = blocks // 2
    channels = dec_out.shape[1]
    steps = samples // STEP
    tiles = cell_tiles.reshape(blocks)
    fields = fields_a.reshape(samples, cell_count)
    weights = jnp.swapaxes(regrid_w, 2, 3).reshape(pairs, 2 * BN, BC)
    smem = pl.BlockSpec(memory_space=pltpu.SMEM)
    vmem = pl.BlockSpec(memory_space=pltpu.VMEM)
    hbm = pl.BlockSpec(memory_space=pltpu.HBM)

    sent = pl.pallas_call(
        head_kernel,
        name="head",
        out_shape=jax.ShapeDtypeStruct((pairs, 2 * samples, nodes), jnp.bfloat16),
        in_specs=[smem, hbm, hbm, hbm, vmem, hbm, hbm],
        out_specs=hbm,
        scratch_shapes=[
            pltpu.VMEM(fields.shape, jnp.bfloat16),
            pltpu.VMEM(latent_b.shape, jnp.bfloat16),
            pltpu.VMEM(weights.shape, jnp.bfloat16),
            pltpu.VMEM(dec_mid.shape, jnp.bfloat16),
            pltpu.VMEM(dec_out.shape, jnp.bfloat16),
            pltpu.VMEM((channels, hidden), jnp.bfloat16),
            pltpu.VMEM((channels, samples, nodes), jnp.float32),
            pltpu.VMEM((pairs, 2 * samples, nodes), jnp.bfloat16),
            pltpu.SemaphoreType.DMA((steps + 12,)),
        ],
        cost_estimate=pl.CostEstimate(flops=3_000_000_000, bytes_accessed=9_000_000, transcendentals=1_000_000),
    )(tiles, fields, latent_b, weights, norm_b.reshape(1, hidden), dec_mid, dec_out)

    got = lax.all_to_all(sent, "ch", split_axis=0, concat_axis=0, tiled=True)

    latent_a, cells = pl.pallas_call(
        tail_kernel,
        name="tail",
        out_shape=(
            jax.ShapeDtypeStruct((samples, nodes, hidden), jnp.bfloat16),
            jax.ShapeDtypeStruct((samples, cell_count), jnp.bfloat16),
        ),
        in_specs=[smem, vmem, hbm, vmem, vmem, vmem, vmem],
        out_specs=(hbm, hbm),
        scratch_shapes=[
            pltpu.VMEM(weights.shape, jnp.bfloat16),
            pltpu.VMEM((channels, samples, nodes), jnp.float32),
            pltpu.VMEM((samples, nodes, hidden), jnp.bfloat16),
            pltpu.VMEM((samples, cell_count), jnp.bfloat16),
            pltpu.SemaphoreType.DMA((steps + 5,)),
        ],
        compiler_params=pltpu.CompilerParams(vmem_limit_bytes=48 * 2**20),
        cost_estimate=pl.CostEstimate(flops=4_000_000_000, bytes_accessed=9_000_000, transcendentals=1_000_000),
    )(tiles, got, weights, norm_a.reshape(channels, 1), enc_in, enc_mid, enc_out)
    return latent_a, cells.reshape(samples, 1, cell_count)


def solution(mesh):
    placed = (P("rep", "ch", None), P("rep", "ch", None)) + (P(),) * 9
    return jax.shard_map(
        shards,
        mesh=mesh,
        in_specs=placed,
        out_specs=(P("rep", "ch", None), P("rep", "ch", None)),
        check_vma=False,
    )
```

time: 81 us -> 61.8 us (0.76)
  matrix products: 16.2 us -> 0 us
  Pallas kernels: 0 us -> 15.6 us
  local copies, waits for them, and re-layouts: 14.4 us -> 0.14 us
  waiting for transfers between devices: 20.4 us -> 30.2 us
  other arithmetic: 8.38 us -> 0 us
  starting transfers between devices: 20.3 us -> 14.9 us
    dot_general x5 -> x0, matrix products: 16.2 us -> none  [the longest x1 4.53 us: shards(): jnp.einsum('ecnj,njm->ecnm', chosen, weights, preferred_element_type=jnp....]
    pallas_call x0 -> x2, Pallas kernels: none -> 15.6 us  [the longest x1 8.9 us: shards(): pl.pallas_call(head_kernel, name='head', out_shape=jax.ShapeDtypeStruct((...]
    all_to_all x2 -> x1, waiting for transfers between devices: 20.4 us -> 30.2 us  [shards(): got = lax.all_to_all(sent, 'ch', split_axis=0, concat_axis=0, tiled=True)]
    gather x3 -> x0, local copies, waits for them, and re-layouts: 6.9 us -> none  [the longest x1 5.21 us: shards(): weight_sel = regrid_w[inverse, jnp.arange(K)[:, None]]]
    all_to_all x2 -> x1, starting transfers between devices: 20.3 us -> 14.9 us  [shards(): got = lax.all_to_all(sent, 'ch', split_axis=0, concat_axis=0, tiled=True)]
    reduce_sum x4 -> x0, other arithmetic: 4.87 us -> none  [the longest x2 2.64 us: normalize(): spread = jnp.mean(centred * centred, axis=along, keepdims=True)]
    sort x1 -> x0, other arithmetic: 3.23 us -> none  [shards(): inverse = jnp.argsort(cell_tiles, axis=0).T]
    reshape x4 -> x1, local copies, waits for them, and re-layouts: 3.33 us -> 0.11 us  [shards(): norm_a.reshape(channels, 1)]
  transfers between devices with their start and end apart: 2 -> 1, of which waited for: 2 -> 1; matrix products, arithmetic and copies ran while one was open for 24% -> 0% of each run, Pallas kernels for 0% -> 0%
where the time goes in v1:
time: 61.8 us; the launch traced here: 61.6 us
  waiting for transfers between devices  30.2 us (49%)
  Pallas kernels  15.6 us (25%)
  starting transfers between devices  14.9 us (24%)
  between operations  0.71 us (1%)
    all_to_all x1, waiting for transfers between devices, shards(): got = lax.all_to_all(sent, 'ch', split_axis=0, concat_axis=0, tiled=True)  30.2 us
    all_to_all x1, starting transfers between devices, shards(): got = lax.all_to_all(sent, 'ch', split_axis=0, concat_axis=0, tiled=True)  14.9 us
    pallas_call x1, Pallas kernels, shards(): pl.pallas_call(head_kernel, name='head', out_shape=jax.ShapeDtypeStruct((...  8.9 us
    pallas_call x1, Pallas kernels, shards(): pl.pallas_call(tail_kernel, name='tail', out_shape=(jax.ShapeDtypeStruct(...  6.72 us
  transfers between devices with their start and end apart: 1, of which 1 were waited for; matrix products, arithmetic and copies ran while one was open for 0% of the time, Pallas kernels for 0%

profile of v1, /device:TPU:1, one launch (start us, length us, event | category | flops | bytes accessed | tf_op | source)
XLA Modules:
  0.0 61.6 jit_solution(16820172642746791317)
XLA Ops:
  0.6 8.9 %head.1 = bf16[128,32,128]{2,1,0:T(8,128)(2,1)} custom-call(s32[256]{0:T(256)} %bitcast.8, bf16[16,32768]{1,0:T(8,128)(2,1)} %bitcast.13, bf16[16,128,512]{2,1,0:T(8,128)(2,1)} %latent.1, bf16[128,128,128]{2,1,0:T(8,128)(2,1)} %bitcast.11, f32[1,512]{1,0:T(1,128)} %bitcast.14, bf16[512,512]{1,0:T(8,128)(2,1)} %mid_w.2, bf16[512,128]{1,0:T(8,128)(2,1)} %out_w.2), custom_call_target="tpu_custom_call" | custom-call | flops 3000000000 | bytes 9000000 | tf_op jit(solution)/shard_map/head/pallas_call | solution.py:207
  9.5 0.0 copy-start.4
  9.5 0.0 copy-start
  9.6 0.0 copy-start.1
  9.6 0.0 copy-start.2
  9.6 0.0 copy-start.3
  9.6 14.9 %all-to-all-start = ((bf16[128,32,128]{2,1,0:T(8,128)(2,1)}), bf16[128,32,128]{2,1,0:T(8,128)(2,1)S(1)}, u32[]{:S(2)}, u32[]{:S(2)}) async-start(bf16[128,32,128]{2,1,0:T(8,128)(2,1)} %head.1), calls=%async_computation | async-start | bytes 2097152 | tf_op jit(solution)/shard_map/all_to_all | solution.py:227
  24.5 0.0 copy-done.4
  24.5 0.1 copy.13.gain
  24.6 30.2 %all-to-all-done.got = bf16[128,32,128]{2,1,0:T(8,128)(2,1)S(1)} async-done(((bf16[128,32,128]{2,1,0:T(8,128)(2,1)}), bf16[128,32,128]{2,1,0:T(8,128)(2,1)S(1)}, u32[]{:S(2)}, u32[]{:S(2)}) %all-to-all-start) | async-done | bytes 1048608 | tf_op jit(solution)/shard_map/all_to_all | solution.py:227
  54.9 0.0 copy-done
  54.9 0.0 copy-done.1
  54.9 0.0 copy-done.2
  54.9 0.0 copy-done.3
  54.9 6.7 %tail.1 = (bf16[16,128,512]{2,1,0:T(8,128)(2,1)}, bf16[16,32768]{1,0:T(8,128)(2,1)}) custom-call(s32[256]{0:T(256)S(1)} %bitcast.9, bf16[128,32,128]{2,1,0:T(8,128)(2,1)S(1)} %all-to-all-done.got, bf16[128,128,128]{2,1,0:T(8,128)(2,1)} %bitcast.12, f32[128,1]{1,0:T(8,128)S(1)} %copy.13.gain, bf16[128,512]{1,0:T(8,128)(2,1)S(1)} %copy-done.2, ...), custom_call_target="tpu_custom_call" | custom-call | flops 4000000000 | bytes 9000000 | tf_op jit(solution)/shard_map/tail/pallas_call | solution.py:229
Async XLA Ops:
  9.5 15.0 %copy-start.4 = (f32[128]{0:T(128)S(1)}, f32[128]{0:T(128)}, u32[]{:S(2)}) copy-start(f32[128]{0:T(128)} %param.15) | copy-start | bytes 1540
  9.5 45.3 %copy-start = (bf16[512,512]{1,0:T(8,128)(2,1)S(1)}, bf16[512,512]{1,0:T(8,128)(2,1)}, u32[]{:S(2)}) copy-start(bf16[512,512]{1,0:T(8,128)(2,1)} %mid_w.3) | copy-start | bytes 1572868
  9.6 45.3 %copy-start.1 = (bf16[512,512]{1,0:T(8,128)(2,1)S(1)}, bf16[512,512]{1,0:T(8,128)(2,1)}, u32[]{:S(2)}) copy-start(bf16[512,512]{1,0:T(8,128)(2,1)} %out_w.3) | copy-start | bytes 1572868
  9.6 45.3 %copy-start.2 = (bf16[128,512]{1,0:T(8,128)(2,1)S(1)}, bf16[128,512]{1,0:T(8,128)(2,1)}, u32[]{:S(2)}) copy-start(bf16[128,512]{1,0:T(8,128)(2,1)} %in_w.1) | copy-start | bytes 393220
  9.6 45.3 %copy-start.3 = (s32[256,1]{0,1:T(1,128)S(1)}, s32[256,1]{0,1:T(1,128)}, u32[]{:S(2)}) copy-start(s32[256,1]{0,1:T(1,128)} %param.14) | copy-start | bytes 3076
  9.6 45.3 %all-to-all-start = ((bf16[128,32,128]{2,1,0:T(8,128)(2,1)}), bf16[128,32,128]{2,1,0:T(8,128)(2,1)S(1)}, u32[]{:S(2)}, u32[]{:S(2)}) async-start(bf16[128,32,128]{2,1,0:T(8,128)(2,1)} %head.1), calls=%async_computation | async-start | bytes 2097152 | tf_op jit(solution)/shard_map/all_to_all | solution.py:227

commit v2 on v1

--- a/solution.py
+++ b/solution.py
@@ -11,8 +11,7 @@
 BC = 128
 EPSILON = 1e-05
 STEP = 8
-DEC = 1
-ENC = 1
+SEND = 2
 
 
 def half_silu(values):
@@ -29,7 +28,8 @@
 
 
 def head_kernel(
-    tiles, fields, latent, weights, gain, mid_w, out_w, sent,
+    tiles_in, fields, latent, weights, gain_in, mid_w, out_w, sent,
+    tiles, gain,
     fields_v, latent_v, weights_v, mid_v, out_v, out_t, turned, sent_v, sems,
 ):
     samples, nodes, hidden = latent.shape
@@ -59,9 +59,13 @@
             sent_v.at[rows, :samples, :], sent.at[rows, :samples, :], sems.at[steps + parts + 4 + i]
         )
 
+    tiles_copy = pltpu.make_async_copy(tiles_in, tiles, sems.at[steps + 2 * parts + 4])
+    gain_copy = pltpu.make_async_copy(gain_in, gain, sems.at[steps + 2 * parts + 5])
+    out_copy.start()
     latent_copy(0).start()
     mid_copy.start()
-    out_copy.start()
+    gain_copy.start()
+    tiles_copy.start()
     for i in range(1, steps):
         latent_copy(i).start()
     fields_copy.start()
@@ -70,6 +74,7 @@
 
     out_copy.wait()
     out_t[...] = out_v[...].T
+    gain_copy.wait()
     scale = gain[...]
 
     def decode(i, carry):
@@ -83,14 +88,15 @@
         ).astype(jnp.bfloat16)
         result = nt_dot(out_t[...], middle)
         for s in range(STEP):
-            turned[:, i * STEP + s, :] = result[:, s * nodes:(s + 1) * nodes]
+            turned[pl.ds(i * STEP + s, turned.shape[0] // samples, stride=samples), :] = result[:, s * nodes:(s + 1) * nodes]
         return carry
 
     mid_copy.wait()
-    lax.fori_loop(0, steps, decode, 0, unroll=DEC)
-    sent_v[:, samples:, :] = turned[...].astype(jnp.bfloat16)
+    lax.fori_loop(0, steps, decode, 0, unroll=1)
+    sent_v[:, samples:, :] = turned[...].astype(jnp.bfloat16).reshape(pairs, samples, nodes)
     decoded_copy.start()
 
+    tiles_copy.wait()
     fields_copy.wait()
     low = lax.broadcasted_iota(jnp.int32, (samples, BC), 1) < BN
 
@@ -116,53 +122,61 @@
 
 
 def tail_kernel(
-    tiles, got, weights, gain, in_w, mid_w, out_w, latent, cells,
+    tiles_in, got, weights, gain, in_w, mid_w, out_w, latent, cells,
+    tiles,
     weights_v, turned, latent_v, cells_v, sems,
 ):
     samples, nodes, hidden = latent.shape
     pairs = weights.shape[0]
     steps = samples // STEP
+    sends = samples // SEND
     parts = 2
     share = pairs // parts
 
     def latent_copy(i):
-        rows = pl.ds(i * STEP, STEP)
+        rows = pl.ds(i * SEND, SEND)
         return pltpu.make_async_copy(latent_v.at[rows], latent.at[rows], sems.at[i])
 
     def weight_copy(i):
         rows = pl.ds(i * share, share)
-        return pltpu.make_async_copy(weights.at[rows], weights_v.at[rows], sems.at[steps + i])
-
-    cells_copy = pltpu.make_async_copy(cells_v, cells, sems.at[steps + parts])
+        return pltpu.make_async_copy(weights.at[rows], weights_v.at[rows], sems.at[sends + i])
+
+    cells_copy = pltpu.make_async_copy(cells_v, cells, sems.at[sends + parts])
+    tiles_copy = pltpu.make_async_copy(tiles_in, tiles, sems.at[sends + parts + 1])
     for i in range(parts):
         weight_copy(i).start()
+    tiles_copy.start()
 
     values = got[:, :samples, :].astype(jnp.float32)
     average = jnp.mean(values, axis=0, keepdims=True)
     centred = values - average
     spread = jnp.mean(centred * centred, axis=0, keepdims=True)
-    turned[...] = centred * lax.rsqrt(spread + EPSILON)
+    turned[...] = (centred * lax.rsqrt(spread + EPSILON)).reshape(turned.shape)
 
     scale = jnp.broadcast_to(gain[...], (pairs, nodes))
 
     def encode(i, carry):
         bases = []
         for s in range(STEP):
-            normed = (turned[:, i * STEP + s, :] * scale).astype(jnp.bfloat16)
+            normed = (turned[pl.ds(i * STEP + s, pairs, stride=samples), :] * scale).astype(jnp.bfloat16)
             bases.append(tn_dot(normed, in_w[...]))
         base = jnp.concatenate(bases, axis=0).astype(jnp.bfloat16)
         middle = half_silu(
             jnp.dot(base, mid_w[...], preferred_element_type=jnp.float32)
         ).astype(jnp.bfloat16)
-        result = base.astype(jnp.float32) + jnp.dot(
-            middle, out_w[...], preferred_element_type=jnp.float32
-        )
-        latent_v[pl.ds(i * STEP, STEP)] = result.astype(jnp.bfloat16).reshape(STEP, nodes, hidden)
-        latent_copy(i).start()
+        for k in range(STEP // SEND):
+            rows = slice(k * SEND * nodes, (k + 1) * SEND * nodes)
+            result = base[rows].astype(jnp.float32) + jnp.dot(
+                middle[rows], out_w[...], preferred_element_type=jnp.float32
+            )
+            place = pl.ds(i * STEP + k * SEND, SEND)
+            latent_v[place] = result.astype(jnp.bfloat16).reshape(SEND, nodes, hidden)
+            latent_copy(i * (STEP // SEND) + k).start()
         return carry
 
-    lax.fori_loop(0, steps // 2, encode, 0, unroll=ENC)
+    lax.fori_loop(0, steps // 2, encode, 0)
     low = lax.broadcasted_iota(jnp.int32, (samples, BC), 1) < BN
+    tiles_copy.wait()
     for part in range(parts):
         weight_copy(part).wait()
 
@@ -181,9 +195,9 @@
         lax.fori_loop(part * share, (part + 1) * share, spread_out, 0, unroll=64)
     cells_copy.start()
 
-    lax.fori_loop(steps // 2, steps, encode, 0, unroll=ENC)
+    lax.fori_loop(steps // 2, steps, encode, 0)
     cells_copy.wait()
-    for i in range(steps):
+    for i in range(sends):
         latent_copy(i).wait()
 
 
@@ -200,7 +214,6 @@
     tiles = cell_tiles.reshape(blocks)
     fields = fields_a.reshape(samples, cell_count)
     weights = jnp.swapaxes(regrid_w, 2, 3).reshape(pairs, 2 * BN, BC)
-    smem = pl.BlockSpec(memory_space=pltpu.SMEM)
     vmem = pl.BlockSpec(memory_space=pltpu.VMEM)
     hbm = pl.BlockSpec(memory_space=pltpu.HBM)
 
@@ -208,18 +221,20 @@
         head_kernel,
         name="head",
         out_shape=jax.ShapeDtypeStruct((pairs, 2 * samples, nodes), jnp.bfloat16),
-        in_specs=[smem, hbm, hbm, hbm, vmem, hbm, hbm],
+        in_specs=[hbm, hbm, hbm, hbm, hbm, hbm, hbm],
         out_specs=hbm,
         scratch_shapes=[
+            pltpu.SMEM(tiles.shape, jnp.int32),
+            pltpu.VMEM((1, hidden), jnp.float32),
             pltpu.VMEM(fields.shape, jnp.bfloat16),
             pltpu.VMEM(latent_b.shape, jnp.bfloat16),
             pltpu.VMEM(weights.shape, jnp.bfloat16),
             pltpu.VMEM(dec_mid.shape, jnp.bfloat16),
             pltpu.VMEM(dec_out.shape, jnp.bfloat16),
             pltpu.VMEM((channels, hidden), jnp.bfloat16),
-            pltpu.VMEM((channels, samples, nodes), jnp.float32),
+            pltpu.VMEM((channels * samples, nodes), jnp.float32),
             pltpu.VMEM((pairs, 2 * samples, nodes), jnp.bfloat16),
-            pltpu.SemaphoreType.DMA((steps + 12,)),
+            pltpu.SemaphoreType.DMA((steps + 10,)),
         ],
         cost_estimate=pl.CostEstimate(flops=3_000_000_000, bytes_accessed=9_000_000, transcendentals=1_000_000),
     )(tiles, fields, latent_b, weights, norm_b.reshape(1, hidden), dec_mid, dec_out)
@@ -233,14 +248,15 @@
             jax.ShapeDtypeStruct((samples, nodes, hidden), jnp.bfloat16),
             jax.ShapeDtypeStruct((samples, cell_count), jnp.bfloat16),
         ),
-        in_specs=[smem, vmem, hbm, vmem, vmem, vmem, vmem],
+        in_specs=[hbm, vmem, hbm, vmem, vmem, vmem, vmem],
         out_specs=(hbm, hbm),
         scratch_shapes=[
+            pltpu.SMEM(tiles.shape, jnp.int32),
             pltpu.VMEM(weights.shape, jnp.bfloat16),
-            pltpu.VMEM((channels, samples, nodes), jnp.float32),
+            pltpu.VMEM((channels * samples, nodes), jnp.float32),
             pltpu.VMEM((samples, nodes, hidden), jnp.bfloat16),
             pltpu.VMEM((samples, cell_count), jnp.bfloat16),
-            pltpu.SemaphoreType.DMA((steps + 5,)),
+            pltpu.SemaphoreType.DMA((samples // SEND + 6,)),
         ],
         compiler_params=pltpu.CompilerParams(vmem_limit_bytes=48 * 2**20),
         cost_estimate=pl.CostEstimate(flops=4_000_000_000, bytes_accessed=9_000_000, transcendentals=1_000_000),

time: 61.8 us -> 60.1 us (0.972)
  Pallas kernels: 15.6 us -> 13.9 us
    pallas_call x1, Pallas kernels: 8.9 us -> 7.99 us  [shards(): pl.pallas_call(head_kernel, name='head', out_shape=jax.ShapeDtypeStruct((...]
    pallas_call x1, Pallas kernels: 6.72 us -> 5.95 us  [shards(): pl.pallas_call(tail_kernel, name='tail', out_shape=(jax.ShapeDtypeStruct(...]
where the time goes in v2:
time: 60.1 us; the launch traced here: 59.9 us
  waiting for transfers between devices  30.2 us (50%)
  starting transfers between devices  14.9 us (25%)
  Pallas kernels  13.9 us (23%)
  between operations  0.71 us (1%)
    all_to_all x1, waiting for transfers between devices, shards(): got = lax.all_to_all(sent, 'ch', split_axis=0, concat_axis=0, tiled=True)  30.2 us
    all_to_all x1, starting transfers between devices, shards(): got = lax.all_to_all(sent, 'ch', split_axis=0, concat_axis=0, tiled=True)  14.9 us
    pallas_call x1, Pallas kernels, shards(): pl.pallas_call(head_kernel, name='head', out_shape=jax.ShapeDtypeStruct((...  7.99 us
    pallas_call x1, Pallas kernels, shards(): pl.pallas_call(tail_kernel, name='tail', out_shape=(jax.ShapeDtypeStruct(...  5.95 us
  transfers between devices with their start and end apart: 1, of which 1 were waited for; matrix products, arithmetic and copies ran while one was open for 0% of the time, Pallas kernels for 0%

profile of v2, /device:TPU:1, one launch (start us, length us, event | category | flops | bytes accessed | tf_op | source)
XLA Modules:
  0.0 59.9 jit_solution(16590428175055523003)
XLA Ops:
  0.6 8.0 %head.1 = bf16[128,32,128]{2,1,0:T(8,128)(2,1)} custom-call(s32[256]{0:T(256)} %bitcast.8, bf16[16,32768]{1,0:T(8,128)(2,1)} %bitcast.13, bf16[16,128,512]{2,1,0:T(8,128)(2,1)} %latent.1, bf16[128,128,128]{2,1,0:T(8,128)(2,1)} %bitcast.11, f32[1,512]{1,0:T(1,128)} %bitcast.14, bf16[512,512]{1,0:T(8,128)(2,1)} %mid_w.2, bf16[512,128]{1,0:T(8,128)(2,1)} %out_w.2), custom_call_target="tpu_custom_call" | custom-call | flops 3000000000 | bytes 9000000 | tf_op jit(solution)/shard_map/head/pallas_call | solution.py:220
  8.6 0.0 copy-start.4
  8.6 0.0 copy-start
  8.6 0.0 copy-start.1
  8.7 0.0 copy-start.2
  8.7 0.0 copy-start.3
  8.7 14.9 %all-to-all-start = ((bf16[128,32,128]{2,1,0:T(8,128)(2,1)}), bf16[128,32,128]{2,1,0:T(8,128)(2,1)S(1)}, u32[]{:S(2)}, u32[]{:S(2)}) async-start(bf16[128,32,128]{2,1,0:T(8,128)(2,1)} %head.1), calls=%async_computation | async-start | bytes 2097152 | tf_op jit(solution)/shard_map/all_to_all | solution.py:242
  23.6 0.0 copy-done.4
  23.6 0.1 copy.13.gain
  23.7 30.2 %all-to-all-done.got = bf16[128,32,128]{2,1,0:T(8,128)(2,1)S(1)} async-done(((bf16[128,32,128]{2,1,0:T(8,128)(2,1)}), bf16[128,32,128]{2,1,0:T(8,128)(2,1)S(1)}, u32[]{:S(2)}, u32[]{:S(2)}) %all-to-all-start) | async-done | bytes 1048608 | tf_op jit(solution)/shard_map/all_to_all | solution.py:242
  54.0 0.0 copy-done
  54.0 0.0 copy-done.1
  54.0 0.0 copy-done.2
  54.0 0.0 copy-done.3
  54.0 6.0 %tail.1 = (bf16[16,128,512]{2,1,0:T(8,128)(2,1)}, bf16[16,32768]{1,0:T(8,128)(2,1)}) custom-call(s32[256]{0:T(256)S(1)} %bitcast.9, bf16[128,32,128]{2,1,0:T(8,128)(2,1)S(1)} %all-to-all-done.got, bf16[128,128,128]{2,1,0:T(8,128)(2,1)} %bitcast.12, f32[128,1]{1,0:T(8,128)S(1)} %copy.13.gain, bf16[128,512]{1,0:T(8,128)(2,1)S(1)} %copy-done.2, ...), custom_call_target="tpu_custom_call" | custom-call | flops 4000000000 | bytes 9000000 | tf_op jit(solution)/shard_map/tail/pallas_call | solution.py:244
Async XLA Ops:
  8.6 15.0 %copy-start.4 = (f32[128]{0:T(128)S(1)}, f32[128]{0:T(128)}, u32[]{:S(2)}) copy-start(f32[128]{0:T(128)} %param.15) | copy-start | bytes 1540
  8.6 45.3 %copy-start = (bf16[512,512]{1,0:T(8,128)(2,1)S(1)}, bf16[512,512]{1,0:T(8,128)(2,1)}, u32[]{:S(2)}) copy-start(bf16[512,512]{1,0:T(8,128)(2,1)} %mid_w.3) | copy-start | bytes 1572868
  8.6 45.3 %copy-start.1 = (bf16[512,512]{1,0:T(8,128)(2,1)S(1)}, bf16[512,512]{1,0:T(8,128)(2,1)}, u32[]{:S(2)}) copy-start(bf16[512,512]{1,0:T(8,128)(2,1)} %out_w.3) | copy-start | bytes 1572868
  8.7 45.3 %copy-start.2 = (bf16[128,512]{1,0:T(8,128)(2,1)S(1)}, bf16[128,512]{1,0:T(8,128)(2,1)}, u32[]{:S(2)}) copy-start(bf16[128,512]{1,0:T(8,128)(2,1)} %in_w.1) | copy-start | bytes 393220
  8.7 45.3 %copy-start.3 = (s32[256,1]{0,1:T(1,128)S(1)}, s32[256,1]{0,1:T(1,128)}, u32[]{:S(2)}) copy-start(s32[256,1]{0,1:T(1,128)} %param.14) | copy-start | bytes 3076
  8.7 45.3 %all-to-all-start = ((bf16[128,32,128]{2,1,0:T(8,128)(2,1)}), bf16[128,32,128]{2,1,0:T(8,128)(2,1)S(1)}, u32[]{:S(2)}, u32[]{:S(2)}) async-start(bf16[128,32,128]{2,1,0:T(8,128)(2,1)} %head.1), calls=%async_computation | async-start | bytes 2097152 | tf_op jit(solution)/shard_map/all_to_all | solution.py:242

commit v3 on v2

--- a/solution.py
+++ b/solution.py
@@ -12,6 +12,8 @@
 EPSILON = 1e-05
 STEP = 8
 SEND = 2
+QUAD = 4
+STACK = 2
 
 
 def half_silu(values):
@@ -35,7 +37,7 @@
     samples, nodes, hidden = latent.shape
     pairs = weights.shape[0]
     steps = samples // STEP
-    parts = 2
+    parts = 1
     share = pairs // parts
 
     def latent_copy(i):
@@ -103,17 +105,24 @@
     for part in range(parts):
         weight_copy(part).wait()
 
-        def regrid(d, carry):
-            first = pl.multiple_of(tiles[2 * d] * BC, BC)
-            second = pl.multiple_of(tiles[2 * d + 1] * BC, BC)
+        def regrid(q, carry):
             chosen = jnp.concatenate(
-                [fields_v[:, pl.ds(first, BC)], fields_v[:, pl.ds(second, BC)]], axis=0
+                [
+                    fields_v[:, pl.ds(pl.multiple_of(tiles[2 * QUAD * q + k] * BC, BC), BC)]
+                    for k in range(2 * QUAD)
+                ],
+                axis=0,
             )
-            both = nt_dot(chosen, weights_v[d])
-            sent_v[d, :samples, :] = jnp.where(low, both[:samples], both[samples:]).astype(jnp.bfloat16)
+            both = nt_dot(chosen, weights_v[pl.ds(q * QUAD, QUAD)].reshape(QUAD * BC, BC))
+            for k in range(QUAD):
+                columns = slice(k * BC, (k + 1) * BC)
+                upper = both[2 * k * samples:(2 * k + 1) * samples, columns]
+                lower = both[(2 * k + 1) * samples:(2 * k + 2) * samples, columns]
+                sent_v[q * QUAD + k, :samples, :] = jnp.where(low, upper, lower).astype(jnp.bfloat16)
             return carry
 
-        lax.fori_loop(part * share, (part + 1) * share, regrid, 0, unroll=64)
+        count = share // QUAD
+        lax.fori_loop(part * count, (part + 1) * count, regrid, 0, unroll=count)
         sent_copy(part).start()
 
     decoded_copy.wait()
@@ -130,7 +139,7 @@
     pairs = weights.shape[0]
     steps = samples // STEP
     sends = samples // SEND
-    parts = 2
+    parts = 1
     share = pairs // parts
 
     def latent_copy(i):
@@ -153,7 +162,7 @@
     spread = jnp.mean(centred * centred, axis=0, keepdims=True)
     turned[...] = (centred * lax.rsqrt(spread + EPSILON)).reshape(turned.shape)
 
-    scale = jnp.broadcast_to(gain[...], (pairs, nodes))
+    scale = jnp.broadcast_to(gain[...], (nodes, pairs)).T
 
     def encode(i, carry):
         bases = []
@@ -180,19 +189,27 @@
     for part in range(parts):
         weight_copy(part).wait()
 
-        def spread_out(d, carry):
-            first = pl.multiple_of(tiles[2 * d] * BC, BC)
-            second = pl.multiple_of(tiles[2 * d + 1] * BC, BC)
-            node = got[d, samples:, :].astype(jnp.float32)
-            stacked = jnp.concatenate(
-                [jnp.where(low, node, 0.0), jnp.where(low, 0.0, node)], axis=0
+        def spread_out(q, carry):
+            rows = []
+            for k in range(STACK):
+                node = got[q * STACK + k, samples:, :].astype(jnp.float32)
+                own = jnp.concatenate(
+                    [jnp.where(low, node, 0.0), jnp.where(low, 0.0, node)], axis=0
+                ).astype(jnp.bfloat16)
+                none = jnp.zeros_like(own)
+                rows.append(jnp.concatenate([own if j == k else none for j in range(STACK)], axis=1))
+            both = jnp.dot(
+                jnp.concatenate(rows, axis=0),
+                weights_v[pl.ds(q * STACK, STACK)].reshape(STACK * BC, BC),
+                preferred_element_type=jnp.float32,
             ).astype(jnp.bfloat16)
-            both = jnp.dot(stacked, weights_v[d], preferred_element_type=jnp.float32).astype(jnp.bfloat16)
-            cells_v[:, pl.ds(first, BC)] = both[:samples]
-            cells_v[:, pl.ds(second, BC)] = both[samples:]
+            for k in range(2 * STACK):
+                place = pl.multiple_of(tiles[2 * STACK * q + k] * BC, BC)
+                cells_v[:, pl.ds(place, BC)] = both[k * samples:(k + 1) * samples]
             return carry
 
-        lax.fori_loop(part * share, (part + 1) * share, spread_out, 0, unroll=64)
+        count = share // STACK
+        lax.fori_loop(part * count, (part + 1) * count, spread_out, 0, unroll=count)
     cells_copy.start()
 
     lax.fori_loop(steps // 2, steps, encode, 0)
@@ -260,7 +277,7 @@
         ],
         compiler_params=pltpu.CompilerParams(vmem_limit_bytes=48 * 2**20),
         cost_estimate=pl.CostEstimate(flops=4_000_000_000, bytes_accessed=9_000_000, transcendentals=1_000_000),
-    )(tiles, got, weights, norm_a.reshape(channels, 1), enc_in, enc_mid, enc_out)
+    )(tiles, got, weights, norm_a.reshape(1, channels), enc_in, enc_mid, enc_out)
     return latent_a, cells.reshape(samples, 1, cell_count)
 
 

time: 60.1 us -> 58.4 us (0.972)
  blocking collectives: 0 us -> 45.3 us
  waiting for transfers between devices: 30.2 us -> 0 us
  starting transfers between devices: 14.9 us -> 0 us
  Pallas kernels: 13.9 us -> 12.2 us
    all_to_all x0 -> x1, blocking collectives: none -> 45.3 us  [shards(): got = lax.all_to_all(sent, 'ch', split_axis=0, concat_axis=0, tiled=True)]
    all_to_all x1 -> x0, waiting for transfers between devices: 30.2 us -> none  [shards(): got = lax.all_to_all(sent, 'ch', split_axis=0, concat_axis=0, tiled=True)]
    all_to_all x1 -> x0, starting transfers between devices: 14.9 us -> none  [shards(): got = lax.all_to_all(sent, 'ch', split_axis=0, concat_axis=0, tiled=True)]
    pallas_call x1, Pallas kernels: 7.99 us -> 6.9 us  [shards(): pl.pallas_call(head_kernel, name='head', out_shape=jax.ShapeDtypeStruct((...]
    pallas_call x1, Pallas kernels: 5.95 us -> 5.34 us  [shards(): pl.pallas_call(tail_kernel, name='tail', out_shape=(jax.ShapeDtypeStruct(...]
  transfers between devices with their start and end apart: 1 -> 0, of which waited for: 1 -> 0; matrix products, arithmetic and copies ran while one was open for 0% -> 0% of each run, Pallas kernels for 0% -> 0%
where the time goes in v3:
time: 58.4 us; the launch traced here: 58.2 us
  blocking collectives  45.3 us (78%)
  Pallas kernels  12.2 us (21%)
  between operations  0.7 us (1%)
    all_to_all x1, blocking collectives, shards(): got = lax.all_to_all(sent, 'ch', split_axis=0, concat_axis=0, tiled=True)  45.3 us
    pallas_call x1, Pallas kernels, shards(): pl.pallas_call(head_kernel, name='head', out_shape=jax.ShapeDtypeStruct((...  6.9 us
    pallas_call x1, Pallas kernels, shards(): pl.pallas_call(tail_kernel, name='tail', out_shape=(jax.ShapeDtypeStruct(...  5.34 us

profile of v3, /device:TPU:1, one launch (start us, length us, event | category | flops | bytes accessed | tf_op | source)
XLA Modules:
  0.0 58.2 jit_solution(9298799122063891741)
XLA Ops:
  0.6 6.9 %head.1 = bf16[128,32,128]{2,1,0:T(8,128)(2,1)} custom-call(s32[256]{0:T(256)} %bitcast.8, bf16[16,32768]{1,0:T(8,128)(2,1)} %bitcast.13, bf16[16,128,512]{2,1,0:T(8,128)(2,1)} %latent.1, bf16[128,128,128]{2,1,0:T(8,128)(2,1)} %bitcast.11, f32[1,512]{1,0:T(1,128)} %bitcast.14, bf16[512,512]{1,0:T(8,128)(2,1)} %mid_w.2, bf16[512,128]{1,0:T(8,128)(2,1)} %out_w.2), custom_call_target="tpu_custom_call" | custom-call | flops 3000000000 | bytes 9000000 | tf_op jit(solution)/shard_map/head/pallas_call | solution.py:237
  7.5 0.0 copy-start
  7.5 0.0 copy-start.1
  7.6 0.0 copy-start.2
  7.6 0.0 copy-start.3
  7.6 0.0 copy-start.4
  7.6 45.3 %all_to_all.5.got = bf16[128,32,128]{2,1,0:T(8,128)(2,1)S(1)} all-to-all(bf16[128,32,128]{2,1,0:T(8,128)(2,1)} %head.1), channel_id=1, replica_groups=mesh['ch'=128,'rep'=2] {'ch'}, dimensions={0} | all-to-all | bytes 2097152 | tf_op jit(solution)/shard_map/all_to_all | solution.py:259
  52.9 0.0 copy-done
  52.9 0.0 copy-done.1
  52.9 0.0 copy-done.2
  52.9 0.0 copy-done.3
  52.9 0.0 copy-done.4
  52.9 5.3 %tail.1 = (bf16[16,128,512]{2,1,0:T(8,128)(2,1)}, bf16[16,32768]{1,0:T(8,128)(2,1)}) custom-call(s32[256]{0:T(256)S(1)} %bitcast.9, bf16[128,32,128]{2,1,0:T(8,128)(2,1)S(1)} %all_to_all.5.got, bf16[128,128,128]{2,1,0:T(8,128)(2,1)} %bitcast.12, f32[1,128]{1,0:T(1,128)S(1)} %bitcast.10, bf16[128,512]{1,0:T(8,128)(2,1)S(1)} %copy-done.2, ...), custom_call_target="tpu_custom_call" | custom-call | flops 4000000000 | bytes 9000000 | tf_op jit(solution)/shard_map/tail/pallas_call | solution.py:261
Async XLA Ops:
  7.5 45.3 %copy-start = (bf16[512,512]{1,0:T(8,128)(2,1)S(1)}, bf16[512,512]{1,0:T(8,128)(2,1)}, u32[]{:S(2)}) copy-start(bf16[512,512]{1,0:T(8,128)(2,1)} %mid_w.3) | copy-start | bytes 1572868
  7.5 45.3 %copy-start.1 = (bf16[512,512]{1,0:T(8,128)(2,1)S(1)}, bf16[512,512]{1,0:T(8,128)(2,1)}, u32[]{:S(2)}) copy-start(bf16[512,512]{1,0:T(8,128)(2,1)} %out_w.3) | copy-start | bytes 1572868
  7.6 45.3 %copy-start.2 = (bf16[128,512]{1,0:T(8,128)(2,1)S(1)}, bf16[128,512]{1,0:T(8,128)(2,1)}, u32[]{:S(2)}) copy-start(bf16[128,512]{1,0:T(8,128)(2,1)} %in_w.1) | copy-start | bytes 393220
  7.6 45.3 %copy-start.3 = (s32[256,1]{0,1:T(1,128)S(1)}, s32[256,1]{0,1:T(1,128)}, u32[]{:S(2)}) copy-start(s32[256,1]{0,1:T(1,128)} %param.14) | copy-start | bytes 3076
  7.6 45.3 %copy-start.4 = (f32[128]{0:T(128)S(1)}, f32[128]{0:T(128)}, u32[]{:S(2)}) copy-start(f32[128]{0:T(128)} %param.15) | copy-start | bytes 1540
